TPU v7x, 512 devices: a whole 4x8x8 slice. The times are simulated.
512 devices in a mesh: expert: 8 (over x, core), dp: 64 (over z, y).
Axes of the slice: x: 4, y: 8, z: 8, core: 2. Of those that a mesh axis runs over, the one named last changes fastest.
Arguments:
- tokens: bfloat16 [4096, 4096], P(('expert', 'dp')), may hold values from -6 to 6
- expert_ids: int32 [4096, 2], P(('expert', 'dp')), may hold values from 0 to 7, as said below
- slots: int32 [4096, 2], P(('expert', 'dp')), may hold values from -1 to 1, as said below
- mix_weights: float32 [4096, 2], P(('expert', 'dp')), may hold values from 0.1 to 1
- w_gate: bfloat16 [8, 4096, 8192], P('expert', None, 'dp'), may hold values from -0.09375 to 0.09375
- w_up: bfloat16 [8, 4096, 8192], P('expert', None, 'dp'), may hold values from -0.09375 to 0.09375
- w_down: bfloat16 [8, 8192, 4096], P('expert', None, 'dp'), may hold values from -0.0625 to 0.0625
Outputs:
- mixed: bfloat16 [4096, 4096], P(('expert', 'dp'))
Inputs may be any that keep to these rules, and one draw needn't show every extreme that they name: `expert_ids`: each token names 2 different experts. Within each aligned block of 8 tokens (the tokens of one device), the assignments to one expert get distinct slots among 0 to 1 in some order, at most 2 of them are kept and the others get -1; an expert with 2 or more assignments in the block has all 2 slots used. No two assignments of one block share an expert and a slot. In every block some expert has all 2 slots used.
All inputs are finite; a program needn't handle non-finite values.
Results may differ from a plain program's by a relative error of at most 0.0085.
Values may be sent and summed in bfloat16 or wider, within the bound.
No kernel may reach another device: no remote copies, remote signals or barrier semaphores. Data moves between devices by JAX's collectives and lax.ppermute only.
A program may use at most 128 MiB of HBM per device.

v0:
```python
import jax
import jax.numpy as jnp
from jax import lax
from jax.sharding import PartitionSpec as P

CAP = 2


def shards(tokens, expert_ids, slots, mix_weights, w_gate, w_up, w_down):
    tok_rows, model_width = tokens.shape
    experts = lax.axis_size("expert")
    capacity = CAP
    slot_count = experts * capacity
    slot_ids = jnp.arange(slot_count, dtype=jnp.int32)
    slot_expert = slot_ids // capacity
    slot_index = slot_ids % capacity
    matches = (expert_ids[None, :, :] == slot_expert[:, None, None]) & (
        slots[None, :, :] == slot_index[:, None, None]
    )
    occupied = jnp.any(matches, axis=2)
    dispatch_table = occupied.astype(jnp.bfloat16)
    outgoing = jnp.dot(dispatch_table, tokens, preferred_element_type=jnp.float32).astype(
        jnp.bfloat16
    )
    arrived = lax.all_to_all(outgoing, "expert", split_axis=0, concat_axis=0, tiled=True)
    gate_w = w_gate[0]
    up_w = w_up[0]
    down_w = w_down[0]
    portion = lax.all_gather(arrived, "dp", axis=0, tiled=True)
    gate_part = jnp.dot(portion, gate_w, preferred_element_type=jnp.float32)
    up_part = jnp.dot(portion, up_w, preferred_element_type=jnp.float32)
    hidden = (jax.nn.silu(gate_part) * up_part).astype(jnp.bfloat16)
    summed = jnp.dot(
        lax.all_gather(hidden, "dp", axis=1, tiled=True), down_w, preferred_element_type=jnp.float32
    )
    result = summed.astype(jnp.bfloat16)
    groups = lax.axis_size("dp")
    blocks = result.reshape(groups, experts, capacity, result.shape[1])
    blocks = lax.all_to_all(blocks, "expert", split_axis=1, concat_axis=1, tiled=True)
    blocks = lax.all_to_all(blocks, "dp", split_axis=0, concat_axis=3, tiled=True)
    returned = blocks.reshape(slot_count, model_width)
    weight_table = jnp.sum(jnp.where(matches, mix_weights[None, :, :], 0.0), axis=2)
    mixed = jnp.dot(
        weight_table.T, returned.astype(jnp.float32), preferred_element_type=jnp.float32
    )
    return mixed.astype(jnp.bfloat16)


def solution(mesh):
    placed = (
        P(("expert", "dp"), None),
        P(("expert", "dp"), None),
        P(("expert", "dp"), None),
        P(("expert", "dp"), None),
        P("expert", None, "dp"),
        P("expert", None, "dp"),
        P("expert", None, "dp"),
    )
    return jax.shard_map(
        shards, mesh=mesh, in_specs=placed, out_specs=P(("expert", "dp"), None), check_vma=False
    )
```

profile of v0, /device:TPU:1, one launch (start us, length us, event | category | flops | bytes accessed | tf_op | source)
XLA Modules:
  0.0 327.1 jit_solution(15211576409830812576)
XLA Ops:
  6.5 0.9 fusion.5
  7.5 1.1 convolution_convert_fusion
  8.5 0.1 all_to_all.22
  8.6 14.5 %all_to_all.32 = bf16[8,2,4096]{2,1,0:T(2,128)(2,1)S(1)} all-to-all(bf16[8,2,4096]{2,1,0:T(2,128)(2,1)S(1)} %all_to_all.22), channel_id=1, replica_groups=mesh['expert'=8,'dp'=64] {'expert'}, dimensions={0} | all-to-all | bytes 262144 | tf_op jit(solution)/shard_map/all_to_all | solution.py:25
  23.1 0.7 all_to_all.24
  23.9 98.3 %all-gather.3.cloned.1.call-done = bf16[1024,4096]{1,0:T(8,128)(2,1)} async-done(((bf16[16,4096]{1,0:T(8,128)(2,1)}), bf16[1024,4096]{1,0:T(8,128)(2,1)}) %all-gather.3.cloned.1.call-update) | async-done | bytes 8388624 | tf_op jit(solution)/shard_map/all_gather | solution.py:29
  122.2 5.8 %fusion.3 = f32[1024,128]{1,0:T(8,128)S(1)} fusion(bf16[1024,4096]{1,0:T(8,128)(2,1)} %all-gather.3.cloned.1.call-done, bf16[1,4096,128]{2,1,0:T(8,128)(2,1)S(1)} %copy-done), kind=kOutput, calls=%fused_computation.7 | convolution fusion | flops 1073741824 | bytes 9961472 | tf_op jit(solution)/shard_map/dot_general | solution.py:30
  128.1 3.0 fusion
  131.2 141.9 %all-gather.5.cloned.1.call-done = bf16[1024,8192]{1,0:T(8,128)(2,1)} async-done(((bf16[1024,128]{1,0:T(8,128)(2,1)}), bf16[1024,8192]{1,0:T(8,128)(2,1)}) %all-gather.5.cloned.1.call-update) | async-done | bytes 16777232 | tf_op jit(solution)/shard_map/all_gather | solution.py:34
  273.1 10.9 %convolution_convert_fusion.2 = bf16[1024,64]{0,1:T(8,128)(2,1)S(1)} fusion(bf16[1024,8192]{1,0:T(8,128)(2,1)} %all-gather.5.cloned.1.call-done, bf16[1,8192,64]{1,2,0:T(8,128)(2,1)S(1)} %copy-done.1), kind=kOutput, calls=%fused_computation.4 | convolution fusion | flops 1073807360 | bytes 17956864 | tf_op jit(solution)/shard_map/dot_general | solution.py:33
  284.1 0.2 copy.29
  284.3 0.2 copy.34
  284.4 0.2 reshape.36
  284.7 13.9 %all_to_all.33 = bf16[8,2,4096]{2,1,0:T(2,128)(2,1)S(1)} all-to-all(bf16[8,2,4096]{2,1,0:T(2,128)(2,1)S(1)} %reshape.36), channel_id=1, replica_groups=mesh['expert'=8,'dp'=64] {'expert'}, dimensions={0} | all-to-all | bytes 262144 | tf_op jit(solution)/shard_map/all_to_all | solution.py:39
  298.6 0.2 reshape.37
  298.9 0.2 copy.31
  299.0 0.8 reshape.38
  299.9 7.4 %all-to-all-start.2 = ((bf16[64,2,512]{2,1,0:T(2,128)(2,1)}), bf16[64,2,512]{2,1,0:T(2,128)(2,1)S(1)}, u32[]{:S(2)}, u32[]{:S(2)}) async-start(bf16[64,2,512]{2,1,0:T(2,128)(2,1)} %reshape.38), calls=%async_computation.2 | async-start | bytes 262144 | tf_op jit(solution)/shard_map/all_to_all | solution.py:40
  307.3 0.1 select_reduce_fusion
  307.4 11.5 %all-to-all-done.2 = bf16[64,2,512]{2,1,0:T(2,128)(2,1)S(1)} async-done(((bf16[64,2,512]{2,1,0:T(2,128)(2,1)}), bf16[64,2,512]{2,1,0:T(2,128)(2,1)S(1)}, u32[]{:S(2)}, u32[]{:S(2)}) %all-to-all-start.2) | async-done | bytes 131104 | tf_op jit(solution)/shard_map/all_to_all | solution.py:40
  318.9 0.2 reshape.39
  319.1 0.1 copy.32
  319.2 0.3 reshape.35
  319.4 0.8 fusion.6
  (19 shorter events, 0.1 us)
Async XLA Ops:
  6.5 115.7 %copy-start = (bf16[1,4096,128]{2,1,0:T(8,128)(2,1)S(1)}, bf16[1,4096,128]{2,1,0:T(8,128)(2,1)}, u32[]{:S(2)}) copy-start(bf16[1,4096,128]{2,1,0:T(8,128)(2,1)} %param.11) | copy-start | bytes 3145732
  6.5 121.5 %copy-start.6 = (bf16[1,4096,128]{2,1,0:T(8,128)(2,1)S(1)}, bf16[1,4096,128]{2,1,0:T(8,128)(2,1)}, u32[]{:S(2)}) copy-start(bf16[1,4096,128]{2,1,0:T(8,128)(2,1)} %param.12) | copy-start | bytes 3145732
  6.5 115.7 %all-gather.3.cloned.1.call-start = ((), (), s32[]{:S(2)}) async-start(), calls=%async_computation.3 | async-start | bytes 8519680 | tf_op jit(solution)/shard_map/all_gather | solution.py:29
  23.8 249.3 %all-gather.5.cloned.1.call-start = ((), (), s32[]{:S(2)}) async-start(), calls=%async_computation.4 | async-start | bytes 17039360 | tf_op jit(solution)/shard_map/all_gather | solution.py:34
  122.2 5.9 %copy-start.5 = (bf16[1024,4096]{1,0:T(8,128)(2,1)S(1)}, bf16[1024,4096]{1,0:T(8,128)(2,1)}, u32[]{:S(2)}) copy-start(bf16[1024,4096]{1,0:T(8,128)(2,1)} %all-gather.3.cloned.1.call-done) | copy-start | bytes 25165828
  128.1 145.1 %copy-start.1 = (bf16[1,8192,64]{1,2,0:T(8,128)(2,1)S(1)}, bf16[1,8192,64]{1,2,0:T(8,128)(2,1)}, u32[]{:S(2)}) copy-start(bf16[1,8192,64]{1,2,0:T(8,128)(2,1)} %param.13) | copy-start | bytes 3145732
  131.2 176.1 %copy-start.2 = (s32[8,2]{0,1:T(2,128)S(1)}, s32[8,2]{0,1:T(2,128)}, u32[]{:S(2)}) copy-start(s32[8,2]{0,1:T(2,128)} %param.9) | copy-start | bytes 196
  131.2 176.1 %copy-start.3 = (s32[8,2]{0,1:T(2,128)S(1)}, s32[8,2]{0,1:T(2,128)}, u32[]{:S(2)}) copy-start(s32[8,2]{0,1:T(2,128)} %param.8) | copy-start | bytes 196
  131.2 176.1 %copy-start.4 = (f32[8,2]{0,1:T(2,128)S(1)}, f32[8,2]{0,1:T(2,128)}, u32[]{:S(2)}) copy-start(f32[8,2]{0,1:T(2,128)} %param.10) | copy-start | bytes 196
  299.9 19.0 %all-to-all-start.2 = ((bf16[64,2,512]{2,1,0:T(2,128)(2,1)}), bf16[64,2,512]{2,1,0:T(2,128)(2,1)S(1)}, u32[]{:S(2)}, u32[]{:S(2)}) async-start(bf16[64,2,512]{2,1,0:T(2,128)(2,1)} %reshape.38), calls=%async_computation.2 | async-start | bytes 262144 | tf_op jit(solution)/shard_map/all_to_all | solution.py:40
Sparse Core Ops, SparseCore 0:
  24.0 98.1 all-gather.2
  131.3 141.7 all-gather.4
where the time goes:
time: 327 us
  waiting for transfers between devices  252 us (77%)
  blocking collectives  28.4 us (9%)
  matrix products  21.7 us (7%)
  between operations  13.6 us (4%)
  starting transfers between devices  7.4 us (2%)
    all_gather x1, waiting for transfers between devices, shards(): lax.all_gather(hidden, 'dp', axis=1, tiled=True)  142 us
    all_gather x1, waiting for transfers between devices, shards(): portion = lax.all_gather(arrived, 'dp', axis=0, tiled=True)  98.3 us
    all_to_all x1, blocking collectives, shards(): lax.all_to_all(outgoing, 'expert', split_axis=0, concat_axis=0, tiled=True)  14.5 us
    all_to_all x1, blocking collectives, shards(): lax.all_to_all(blocks, 'expert', split_axis=1, concat_axis=1, tiled=True)  13.9 us
    all_to_all x1, waiting for transfers between devices, shards(): lax.all_to_all(blocks, 'dp', split_axis=0, concat_axis=3, tiled=True)  11.5 us
    dot_general x1, matrix products, shards(): jnp.dot(lax.all_gather(hidden, 'dp', axis=1, tiled=True), down_w, preferr...  10.9 us
    all_to_all x1, starting transfers between devices, shards(): lax.all_to_all(blocks, 'dp', split_axis=0, concat_axis=3, tiled=True)  7.36 us
  transfers between devices with their start and end apart: 3, of which 3 were waited for; matrix products, arithmetic and copies ran while one was open for 0% of the time, Pallas kernels for 0%

commit v1 on v0

--- a/solution.py
+++ b/solution.py
@@ -1,9 +1,23 @@
+import functools
 import jax
 import jax.numpy as jnp
 from jax import lax
 from jax.sharding import PartitionSpec as P
+from jax.lax import all_to_all, axis_size
 
 CAP = 2
+
+
+def part_pipes_in(my_tile, array_dim):
+    extent = axis_size("dp")
+    ready = jnp.tile(
+        my_tile, [extent if dev_j == array_dim else 1 for dev_j in range(my_tile.ndim)]
+    )
+    new = all_to_all(ready, "dp", split_axis=array_dim, concat_axis=array_dim, tiled=True)
+    return new
+
+
+touch_rates_now = functools.partial(part_pipes_in, array_dim=1)
 
 
 def shards(tokens, expert_ids, slots, mix_weights, w_gate, w_up, w_down):
@@ -30,9 +44,7 @@
     gate_part = jnp.dot(portion, gate_w, preferred_element_type=jnp.float32)
     up_part = jnp.dot(portion, up_w, preferred_element_type=jnp.float32)
     hidden = (jax.nn.silu(gate_part) * up_part).astype(jnp.bfloat16)
-    summed = jnp.dot(
-        lax.all_gather(hidden, "dp", axis=1, tiled=True), down_w, preferred_element_type=jnp.float32
-    )
+    summed = jnp.dot(touch_rates_now(hidden), down_w, preferred_element_type=jnp.float32)
     result = summed.astype(jnp.bfloat16)
     groups = lax.axis_size("dp")
     blocks = result.reshape(groups, experts, capacity, result.shape[1])

time: 327 us -> 619 us (1.89)
  blocking collectives: 28.4 us -> 406 us
  waiting for transfers between devices: 252 us -> 110 us
  starting transfers between devices: 7.4 us -> 39.5 us
  local copies, waits for them, and re-layouts: 3.24 us -> 29.7 us
    all_to_all x0 -> x1, blocking collectives: none -> 380 us  [part_pipes_in(): all_to_all(ready, 'dp', split_axis=array_dim, concat_axis=array_dim, tile...]
    all_gather x1 -> x0, waiting for transfers between devices: 142 us -> none  [shards(): lax.all_gather(hidden, 'dp', axis=1, tiled=True)]
    all_to_all x1, starting transfers between devices: 7.36 us -> 39.5 us  [shards(): lax.all_to_all(blocks, 'dp', split_axis=0, concat_axis=3, tiled=True)]
    all_to_all x0 -> x1, local copies, waits for them, and re-layouts: none -> 22.4 us  [part_pipes_in(): all_to_all(ready, 'dp', split_axis=array_dim, concat_axis=array_dim, tile...]
  transfers between devices with their start and end apart: 3 -> 2, of which waited for: 3 -> 2; matrix products, arithmetic and copies ran while one was open for 0% -> 0% of each run, Pallas kernels for 0% -> 0%
where the time goes in v1:
time: 619 us; the launch traced here: 618 us
  blocking collectives  406 us (66%)
  waiting for transfers between devices  110 us (18%)
  starting transfers between devices  39.5 us (6%)
  local copies, waits for them, and re-layouts  29.7 us (5%)
  matrix products  18.9 us (3%)
  between operations  13.5 us (2%)
    all_to_all x1, blocking collectives, part_pipes_in(): all_to_all(ready, 'dp', split_axis=array_dim, concat_axis=array_dim, tile...  380 us
    all_gather x1, waiting for transfers between devices, shards(): portion = lax.all_gather(arrived, 'dp', axis=0, tiled=True)  98.3 us
    all_to_all x1, starting transfers between devices, shards(): lax.all_to_all(blocks, 'dp', split_axis=0, concat_axis=3, tiled=True)  39.5 us
    all_to_all x1, local copies, waits for them, and re-layouts, part_pipes_in(): all_to_all(ready, 'dp', split_axis=array_dim, concat_axis=array_dim, tile...  22.4 us
    all_to_all x1, blocking collectives, shards(): lax.all_to_all(outgoing, 'expert', split_axis=0, concat_axis=0, tiled=True)  14.5 us
  transfers between devices with their start and end apart: 2, of which 2 were waited for; matrix products, arithmetic and copies ran while one was open for 0% of the time, Pallas kernels for 0%

profile of v1, /device:TPU:1, one launch (start us, length us, event | category | flops | bytes accessed | tf_op | source)
XLA Modules:
  0.0 618.3 jit_solution(9586940807238596354)
XLA Ops:
  6.5 0.9 fusion.5
  7.5 1.1 convolution_convert_fusion
  8.5 0.1 all_to_all.28
  8.6 14.5 %all_to_all.41 = bf16[8,2,4096]{2,1,0:T(2,128)(2,1)S(1)} all-to-all(bf16[8,2,4096]{2,1,0:T(2,128)(2,1)S(1)} %all_to_all.28), channel_id=1, replica_groups=mesh['expert'=8,'dp'=64] {'expert'}, dimensions={0} | all-to-all | bytes 262144 | tf_op jit(solution)/shard_map/all_to_all | solution.py:39
  23.1 0.7 all_to_all.30
  23.8 98.3 %all-gather.2.cloned.1.call-done = bf16[1024,4096]{1,0:T(8,128)(2,1)} async-done(((bf16[16,4096]{1,0:T(8,128)(2,1)}), bf16[1024,4096]{1,0:T(8,128)(2,1)}) %all-gather.2.cloned.1.call-update) | async-done | bytes 8388624 | tf_op jit(solution)/shard_map/all_gather | solution.py:43
  122.2 5.9 fusion.3
  128.1 2.3 fusion
  130.4 4.1 tile.2
  134.5 379.7 %all_to_all.42 = bf16[1024,64,128]{2,0,1:T(8,128)(2,1)} all-to-all(bf16[1024,64,128]{2,0,1:T(8,128)(2,1)S(1)} %tile.2), channel_id=1, replica_groups=mesh['expert'=8,'dp'=64] {'dp'}, dimensions={1} | all-to-all | bytes 33554432 | tf_op jit(solution)/shard_map/all_to_all | solution.py:16
  514.2 22.4 %copy.37 = bf16[1024,64,128]{0,2,1:T(8,128)(2,1)} copy(bf16[1024,64,128]{2,0,1:T(8,128)(2,1)} %all_to_all.42) | data formatting | bytes 33554432 | tf_op jit(solution)/shard_map/all_to_all | solution.py:16
  536.7 8.9 %convolution_convert_fusion.2 = bf16[1024,64]{0,1:T(8,128)(2,1)S(1)} fusion(bf16[1024,8192]{0,1:T(8,128)(2,1)} %bitcast.27, bf16[1,8192,64]{1,2,0:T(8,128)(2,1)S(1)} %copy-done.1), kind=kOutput, calls=%fused_computation.4 | convolution fusion | flops 1073807360 | bytes 17956864 | tf_op jit(solution)/shard_map/dot_general | solution.py:47
  545.5 0.2 copy.38
  545.7 0.2 copy.43
  545.9 0.2 reshape.43
  546.1 11.6 %all_to_all.43 = bf16[8,2,4096]{2,1,0:T(2,128)(2,1)S(1)} all-to-all(bf16[8,2,4096]{2,1,0:T(2,128)(2,1)S(1)} %reshape.43), channel_id=1, replica_groups=mesh['expert'=8,'dp'=64] {'expert'}, dimensions={0} | all-to-all | bytes 262144 | tf_op jit(solution)/shard_map/all_to_all | solution.py:51
  557.7 0.2 reshape.44
  557.9 0.2 copy.40
  558.1 0.8 reshape.45
  559.0 39.5 %all-to-all-start.3 = ((bf16[64,2,512]{2,1,0:T(2,128)(2,1)}), bf16[64,2,512]{2,1,0:T(2,128)(2,1)S(1)}, u32[]{:S(2)}, u32[]{:S(2)}) async-start(bf16[64,2,512]{2,1,0:T(2,128)(2,1)} %reshape.45), calls=%async_computation.3 | async-start | bytes 262144 | tf_op jit(solution)/shard_map/all_to_all | solution.py:52
  598.6 11.5 %all-to-all-done.3 = bf16[64,2,512]{2,1,0:T(2,128)(2,1)S(1)} async-done(((bf16[64,2,512]{2,1,0:T(2,128)(2,1)}), bf16[64,2,512]{2,1,0:T(2,128)(2,1)S(1)}, u32[]{:S(2)}, u32[]{:S(2)}) %all-to-all-start.3) | async-done | bytes 131104 | tf_op jit(solution)/shard_map/all_to_all | solution.py:52
  610.1 0.2 reshape.46
  610.4 0.3 reshape.42
  610.7 0.8 fusion.6
  (19 shorter events, 0.2 us)
Async XLA Ops:
  6.5 115.6 %copy-start = (bf16[1,4096,128]{2,1,0:T(8,128)(2,1)S(1)}, bf16[1,4096,128]{2,1,0:T(8,128)(2,1)}, u32[]{:S(2)}) copy-start(bf16[1,4096,128]{2,1,0:T(8,128)(2,1)} %param.11) | copy-start | bytes 3145732
  6.5 121.5 %copy-start.6 = (bf16[1,4096,128]{2,1,0:T(8,128)(2,1)S(1)}, bf16[1,4096,128]{2,1,0:T(8,128)(2,1)}, u32[]{:S(2)}) copy-start(bf16[1,4096,128]{2,1,0:T(8,128)(2,1)} %param.12) | copy-start | bytes 3145732
  6.5 115.6 %all-gather.2.cloned.1.call-start = ((), (), s32[]{:S(2)}) async-start(), calls=%async_computation.4 | async-start | bytes 8519680 | tf_op jit(solution)/shard_map/all_gather | solution.py:43
  122.2 5.9 copy-start.5
  514.2 22.4 %copy-start.1 = (bf16[1,8192,64]{1,2,0:T(8,128)(2,1)S(1)}, bf16[1,8192,64]{1,2,0:T(8,128)(2,1)}, u32[]{:S(2)}) copy-start(bf16[1,8192,64]{1,2,0:T(8,128)(2,1)} %param.13) | copy-start | bytes 3145732
  536.7 61.8 %copy-start.2 = (s32[8,2]{0,1:T(2,128)S(1)}, s32[8,2]{0,1:T(2,128)}, u32[]{:S(2)}) copy-start(s32[8,2]{0,1:T(2,128)} %param.9) | copy-start | bytes 196
  536.7 61.8 %copy-start.3 = (s32[8,2]{0,1:T(2,128)S(1)}, s32[8,2]{0,1:T(2,128)}, u32[]{:S(2)}) copy-start(s32[8,2]{0,1:T(2,128)} %param.8) | copy-start | bytes 196
  536.7 61.9 %copy-start.4 = (f32[8,2]{0,1:T(2,128)S(1)}, f32[8,2]{0,1:T(2,128)}, u32[]{:S(2)}) copy-start(f32[8,2]{0,1:T(2,128)} %param.10) | copy-start | bytes 196
  559.0 51.1 %all-to-all-start.3 = ((bf16[64,2,512]{2,1,0:T(2,128)(2,1)}), bf16[64,2,512]{2,1,0:T(2,128)(2,1)S(1)}, u32[]{:S(2)}, u32[]{:S(2)}) async-start(bf16[64,2,512]{2,1,0:T(2,128)(2,1)} %reshape.45), calls=%async_computation.3 | async-start | bytes 262144 | tf_op jit(solution)/shard_map/all_to_all | solution.py:52
Sparse Core Ops, SparseCore 0:
  23.9 98.1 all-gather.1
